TPU v7x, 32 devices: a whole 2x2x4 slice. The times are simulated.
32 devices in a mesh: band: 8 (over z, x), sub: 4 (over y, core).
Axes of the slice: x: 2, y: 2, z: 4, core: 2. Of those that a mesh axis runs over, the one named last changes fastest.
Arguments:
- grad_pred: bfloat16 [227, 24576], P(None, ('band', 'sub')), may hold values from -6 to 6
- grid_latent: bfloat16 [24576, 512], P(('band', 'sub')), may hold values from -6 to 6
- mesh_latent: bfloat16 [10240, 512], P(('band', 'sub')), may hold values from -6 to 6
- send_slot: int32 [24576], P(('band', 'sub')), may hold values from 0 to 2303, as said below
- edge_src: int32 [3, 73728], P(None, ('band', 'sub')), may hold values from 0 to 10239, as said below
- w_mesh: bfloat16 [512, 512], replicated, may hold values from -0.25 to 0.25
- w_grid: bfloat16 [512, 512], replicated, may hold values from -0.25 to 0.25
- w_msg: bfloat16 [512, 512], replicated, may hold values from -0.25 to 0.25
- w_out: bfloat16 [512, 227], replicated, may hold values from -0.25 to 0.25
Outputs:
- mesh_grad: bfloat16 [10240, 512], P(('band', 'sub'))
- grad_w_mesh: float32 [512, 512], replicated
- grad_w_grid: float32 [512, 512], replicated
- grad_w_msg: float32 [512, 512], replicated
- grad_w_out: float32 [512, 227], replicated
Inputs may be any that keep to these rules, and one draw needn't show every extreme that they name: For grid point p on latitude-major device i, send_slot[p] = j * 72 + r names patch-major device j and a rank r. On one device i the values are distinct, and for each j the ranks used are 0 to the count of i's points sent to j minus 1. Every such count is at most 72, and 72 is reached in every draw. Every grid point thereby gets one patch-major slot; live slots of each source stand at the front of its block of 72. One patch-major device holds at most 1920 live slots, reached on some device in every draw. `edge_src`: A slot on patch-major device j, of band b = j // 4, names senders in patch b only: mesh rows b * 1280 to (b + 1) * 1280 - 1. Entries of empty slots lie in that range too and are not read.
All inputs are finite; a program needn't handle non-finite values.
Results may differ from a plain program's by a relative error of at most 0.0076.
Values may be sent and summed in bfloat16 or wider, within the bound.
No kernel may reach another device: no remote copies, remote signals or barrier semaphores. Data moves between devices by JAX's collectives and lax.ppermute only.
A program may use at most 128 MiB of HBM per device.

v0:
```python
import math
import jax
import jax.numpy as jnp
from jax import lax
from jax.sharding import PartitionSpec as P


def latitude_weight(points, total):
    angle = jnp.pi * ((points.astype(jnp.float32) + 0.5) / total - 0.5)
    return 0.5 * jnp.pi * jnp.cos(angle)


def silu_slope(value):
    sigma = jax.nn.sigmoid(value)
    return sigma * (1.0 + value * (1.0 - sigma))


def contract_rows(left, right):
    return lax.dot_general(
        left, right, (((0,), (0,)), ((), ())), preferred_element_type=jnp.float32
    )


def times_transpose(left, right):
    return lax.dot_general(
        left, right, (((1,), (1,)), ((), ())), preferred_element_type=jnp.float32
    )


def shards(grad_pred, grid_latent, mesh_latent, send_slot, edge_src, w_mesh, w_grid, w_msg, w_out):
    grid_rows = grid_latent.shape[0]
    width = grid_latent.shape[1]
    channels = grad_pred.shape[0]
    devices = lax.axis_size(("band", "sub"))
    capacity = 3 * grid_rows // devices
    total_points = grid_rows * devices
    own_index = lax.axis_index(("band", "sub"))
    points = own_index * grid_rows + jnp.arange(grid_rows, dtype=jnp.int32)
    weighted = (
        latitude_weight(points, total_points)[None, :] * grad_pred.astype(jnp.float32)
    ).astype(jnp.bfloat16)
    target = send_slot // capacity
    slot_rank = send_slot % capacity
    joined = jnp.concatenate([grid_latent, weighted.T], axis=1)
    row_width = width + channels
    send_buffer = (
        jnp.zeros((devices, capacity, row_width), jnp.bfloat16).at[target, slot_rank].set(joined)
    )
    received = lax.all_to_all(send_buffer, ("band", "sub"), split_axis=0, concat_axis=0, tiled=True)
    slots = devices * capacity
    slot_rows = received.reshape(slots, row_width)
    latent_rows = slot_rows[:, :width]
    grad_rows = slot_rows[:, width:]
    grid_proj = jnp.dot(latent_rows, w_grid, preferred_element_type=jnp.float32).astype(
        jnp.bfloat16
    )
    mesh_proj = jnp.dot(mesh_latent, w_mesh, preferred_element_type=jnp.float32).astype(
        jnp.bfloat16
    )
    patch_proj = lax.all_gather(mesh_proj, "sub", axis=0, tiled=True)
    patch_size = patch_proj.shape[0]
    band_index = lax.axis_index("band")
    local_node = edge_src - band_index * patch_size
    grid_float = grid_proj.astype(jnp.float32)
    pre_acts = [
        patch_proj[local_node[corner]].astype(jnp.float32) + grid_float for corner in range(3)
    ]
    act_sum = (
        jax.nn.silu(pre_acts[0]) + jax.nn.silu(pre_acts[1]) + jax.nn.silu(pre_acts[2])
    ).astype(jnp.bfloat16)
    aggregate = jnp.dot(act_sum, w_msg, preferred_element_type=jnp.float32).astype(jnp.bfloat16)
    out_part = contract_rows(aggregate, grad_rows)
    agg_rows = times_transpose(grad_rows, w_out).astype(jnp.bfloat16)
    msg_part = contract_rows(act_sum, agg_rows)
    out_total = lax.psum(out_part, ("band", "sub"))
    msg_total = lax.psum(msg_part, ("band", "sub"))
    act_grad = times_transpose(agg_rows, w_msg)
    pre_grads = [(act_grad * silu_slope(pre)).astype(jnp.bfloat16) for pre in pre_acts]
    grid_proj_grad = (
        pre_grads[0].astype(jnp.float32)
        + pre_grads[1].astype(jnp.float32)
        + pre_grads[2].astype(jnp.float32)
    ).astype(jnp.bfloat16)
    node_part = jnp.zeros((patch_size, width), jnp.float32)
    for corner in range(3):
        node_part = node_part.at[local_node[corner]].add(pre_grads[corner].astype(jnp.float32))
    node_total = lax.psum_scatter(node_part, "sub", scatter_dimension=0, tiled=True)
    grid_part = contract_rows(latent_rows, grid_proj_grad)
    mesh_proj_grad = node_total.astype(jnp.bfloat16)
    mesh_grad = times_transpose(mesh_proj_grad, w_mesh).astype(jnp.bfloat16)
    mesh_part = contract_rows(mesh_latent, mesh_proj_grad)
    grad_scale = 1.0 / math.sqrt(3.0 * total_points)
    grid_total = lax.psum(grid_part, ("band", "sub"))
    mesh_total = lax.psum(mesh_part, ("band", "sub"))
    return (
        mesh_grad,
        mesh_total * grad_scale,
        grid_total * grad_scale,
        msg_total * grad_scale,
        out_total * grad_scale,
    )


def solution(mesh):
    placed = (
        P(None, ("band", "sub")),
        P(("band", "sub"), None),
        P(("band", "sub"), None),
        P(("band", "sub")),
        P(None, ("band", "sub")),
        P(),
        P(),
        P(),
        P(),
    )
    return jax.shard_map(
        shards,
        mesh=mesh,
        in_specs=placed,
        out_specs=(P(("band", "sub"), None), P(), P(), P(), P()),
        check_vma=False,
    )
```

profile of v0, /device:TPU:0, one launch (start us, length us, event | category | flops | bytes accessed | tf_op | source)
XLA Modules:
  0.0 467.4 jit_solution(4389432427457058807)
XLA Ops:
  7.2 0.8 compare_select_fusion.4
  8.0 1.0 fusion.15
  9.2 1.2 pad_maximum_fusion
  10.5 2.0 broadcast_in_dim.9
  12.5 101.6 %scatter_fusion = bf16[32,72,739]{2,1,0:T(8,128)(2,1)} fusion(bf16[32,72,739]{2,1,0:T(8,128)(2,1)} %broadcast_in_dim.9, s32[768]{0:T(1024)S(1)} %fusion.23, bf16[768,739]{1,0:T(8,128)(2,1)S(1)} %pad_maximum_fusion), kind=kCustom, calls=%fused_computation.3 | custom fusion | bytes 3411456 | tf_op jit(solution)/shard_map/scatter | solution.py:47
  114.1 7.4 %all-to-all-start = ((bf16[32,72,739]{2,1,0:T(8,128)(2,1)}), bf16[32,72,739]{2,1,0:T(8,128)(2,1)}, u32[]{:S(2)}, u32[]{:S(2)}) async-start(bf16[32,72,739]{2,1,0:T(8,128)(2,1)} %scatter_fusion), calls=%async_computation | async-start | bytes 7077888 | tf_op jit(solution)/shard_map/all_to_all | solution.py:49
  121.6 1.1 convolution_convert_fusion.4
  122.9 33.9 %all-gather.2.cloned.1.call-done = bf16[1280,512]{1,0:T(8,128)(2,1)} async-done(((bf16[320,512]{1,0:T(8,128)(2,1)}), bf16[1280,512]{1,0:T(8,128)(2,1)}) %all-gather.2.cloned.1.call-update) | async-done | bytes 1310736 | tf_op jit(solution)/shard_map/all_gather | solution.py:60
  156.9 9.2 %gather_fusion.2 = bf16[2304,512]{1,0:T(8,128)(2,1)} fusion(bf16[1280,512]{1,0:T(8,128)(2,1)} %all-gather.2.cloned.1.call-done, s32[3072]{0:T(1024)S(1)} %get-tuple-element.33), kind=kCustom, calls=%fused_computation.2 | custom fusion | bytes 4727808 | tf_op jit(solution)/shard_map/gather | solution.py:66
  166.1 7.5 %gather_fusion.1 = bf16[2304,512]{1,0:T(8,128)(2,1)} fusion(bf16[1280,512]{1,0:T(8,128)(2,1)S(1)} %copy-done.1, s32[3072]{0:T(1024)S(1)} %get-tuple-element.34), kind=kCustom, calls=%fused_computation.1 | custom fusion | bytes 4727808 | tf_op jit(solution)/shard_map/gather | solution.py:66
  173.6 7.5 %gather_fusion = bf16[2304,512]{1,0:T(8,128)(2,1)} fusion(bf16[1280,512]{1,0:T(8,128)(2,1)S(1)} %copy-done.1, s32[3072]{0:T(1024)S(1)} %pad_clamp_fusion.2), kind=kCustom, calls=%fused_computation | custom fusion | bytes 4727808 | tf_op jit(solution)/shard_map/gather | solution.py:66
  181.1 20.5 %all-to-all-done = bf16[32,72,739]{2,1,0:T(8,128)(2,1)} async-done(((bf16[32,72,739]{2,1,0:T(8,128)(2,1)}), bf16[32,72,739]{2,1,0:T(8,128)(2,1)}, u32[]{:S(2)}, u32[]{:S(2)}) %all-to-all-start) | async-done | bytes 3405344 | tf_op jit(solution)/shard_map/all_to_all | solution.py:49
  201.6 2.0 convolution_convert_fusion.2
  203.7 3.9 convolution_convert_fusion.1
  208.4 9.1 %multiply_convert_fusion = (bf16[2304,512]{1,0:T(8,128)(2,1)}, bf16[2304,512]{1,0:T(8,128)(2,1)}, bf16[2304,512]{1,0:T(8,128)(2,1)}, bf16[2304,512]{1,0:T(8,128)(2,1)}) fusion(bf16[2304,512]{1,0:T(8,128)(2,1)S(1)} %convolution_convert_fusion.1, bf16[2304,512]{1,0:T(8,128)(2,1)S(1)} %copy-done.6, bf16[2304,512]{1,0:T(8,128)(2,1)S(1)} %copy-done.7, ...), kind=kOutput, calls=%fused_computation.20 | convolution fusion | flops 1255145472 | bytes 21757952 | tf_op jit(solution)/shard_map/dot_general | solution.py:25
  217.4 17.0 %scatter_custom_fusion.1 = f32[1280,512]{1,0:T(8,128)S(1)} fusion(s32[2304]{0:T(1024)S(1)} %get-tuple-element.22, bf16[2304,512]{1,0:T(8,128)(2,1)} %get-tuple-element.30, f32[]{:T(128)} %constant.20.clone.1), kind=kCustom, calls=%fused_computation.16 | custom fusion | flops 2359296 | bytes 4980740 | tf_op jit(solution)/shard_map/scatter-add | solution.py:86
  234.5 17.5 %scatter_custom_fusion.2 = f32[1280,512]{1,0:T(8,128)S(1)} fusion(f32[1280,512]{1,0:T(8,128)S(1)} %scatter_custom_fusion.1, s32[2304]{0:T(1024)S(1)} %get-tuple-element.21, bf16[2304,512]{1,0:T(8,128)(2,1)} %get-tuple-element.28), kind=kCustom, calls=%fused_computation.14 | custom fusion | flops 2359296 | bytes 4980736 | tf_op jit(solution)/shard_map/scatter-add | solution.py:86
  252.0 17.4 %scatter_custom_fusion.3 = f32[1280,512]{1,0:T(8,128)S(1)} fusion(f32[1280,512]{1,0:T(8,128)S(1)} %scatter_custom_fusion.2, s32[2304]{0:T(1024)S(1)} %get-tuple-element.20, bf16[2304,512]{1,0:T(8,128)(2,1)} %get-tuple-element.27), kind=kCustom, calls=%fused_computation.11 | custom fusion | flops 2359296 | bytes 4980736 | tf_op jit(solution)/shard_map/scatter-add | solution.py:86
  269.4 1.5 copy-done.2
  271.2 4.8 %fusion.24 = f32[512,512]{0,1:T(8,128)} fusion(bf16[2304,512]{1,0:T(8,128)(2,1)} %get-tuple-element.29, bf16[2304,512]{1,0:T(8,128)(2,1)} %copy-done.5), kind=kOutput, calls=%fused_computation.74 | convolution fusion | flops 1207959552 | bytes 5767168 | tf_op jit(solution)/shard_map/dot_general | solution.py:19
  275.9 5.0 %fusion.12 = f32[512,227]{0,1:T(8,128)} fusion(bf16[2304,739]{1,0:T(8,128)(2,1)} %bitcast.2, bf16[2304,512]{1,0:T(8,128)(2,1)} %get-tuple-element.29, bf16[512,512]{1,0:T(8,128)(2,1)S(1)} %copy-done), kind=kOutput, calls=%fused_computation.37 | convolution fusion | flops 1744699392 | bytes 4528128 | tf_op jit(solution)/shard_map/dot_general | solution.py:19
  280.9 5.5 %fusion.7 = f32[512,512]{0,1:T(8,128)} fusion(bf16[2304,512]{1,0:T(8,128)(2,1)} %get-tuple-element.27, bf16[2304,512]{1,0:T(8,128)(2,1)} %get-tuple-element.28, bf16[2304,512]{1,0:T(8,128)(2,1)S(1)} %copy-done.4, bf16[2304,739]{1,0:T(8,128)(2,1)} %bitcast.2), kind=kOutput, calls=%fused_computation.29 | convolution fusion | flops 1215037440 | bytes 10485760 | tf_op jit(solution)/shard_map/dot_general | solution.py:19
  286.5 19.3 %reduce-scatter.2.cloned.1.call-done = f32[320,512]{1,0:T(8,128)} async-done(((f32[1280,512]{1,0:T(8,128)}), f32[320,512]{1,0:T(8,128)}) %reduce-scatter.2.cloned.1.call-update) | async-done | bytes 655376 | tf_op jit(solution)/shard_map/reduce_scatter | solution.py:87
  305.8 2.6 convolution_bitcast_fusion
  308.4 1.1 convolution_convert_fusion.3
  309.5 143.8 %all-reduce.3.cloned.1.call-done = (f32[512,512]{0,1:T(8,128)}, f32[512,512]{0,1:T(8,128)}, f32[512,512]{0,1:T(8,128)}, f32[512,227]{0,1:T(8,128)}) async-done(((f32[512,512]{0,1:T(8,128)}, f32[512,512]{0,1:T(8,128)}, f32[512,512]{0,1:T(8,128)}, f32[512,227]{0,1:T(8,128)}), (f32[512,512]{0,1:T(8,128)}, f32[512,512]{0,1:T(8,128)}, f32[512,512]{0,1:T(8,128)}, ...) | async-done | bytes 3610640 | tf_op jit(solution)/shard_map/psum | solution.py:94
  453.3 1.4 broadcast_multiply_fusion.2
  454.7 1.3 copy.29
  456.0 0.8 broadcast_multiply_fusion.3
  456.8 1.3 broadcast_multiply_fusion.1
  458.2 1.3 copy.30
  459.6 1.3 copy.31
  (47 shorter events, 1.6 us)
Async XLA Ops:
  7.2 200.5 %copy-start = (bf16[512,512]{1,0:T(8,128)(2,1)S(1)}, bf16[512,512]{1,0:T(8,128)(2,1)}, u32[]{:S(2)}) copy-start(bf16[512,512]{1,0:T(8,128)(2,1)} %param.16) | copy-start | bytes 1572868
  114.1 7.5 %copy-start.9 = (bf16[512,512]{1,0:T(8,128)(2,1)S(1)}, bf16[512,512]{1,0:T(8,128)(2,1)}, u32[]{:S(2)}) copy-start(bf16[512,512]{1,0:T(8,128)(2,1)} %param.14) | copy-start | bytes 1572868
  114.1 7.5 %copy-start.11 = (bf16[320,512]{1,0:T(8,128)(2,1)S(1)}, bf16[320,512]{1,0:T(8,128)(2,1)}, u32[]{:S(2)}) copy-start(bf16[320,512]{1,0:T(8,128)(2,1)} %param.11) | copy-start | bytes 983044
  114.1 8.7 %copy-start.15 = (s32[3,2304]{1,0:T(4,128)S(1)}, s32[3,2304]{1,0:T(4,128)}, u32[]{:S(2)}) copy-start(s32[3,2304]{1,0:T(4,128)} %param.13) | copy-start | bytes 82948
  114.1 87.5 %all-to-all-start = ((bf16[32,72,739]{2,1,0:T(8,128)(2,1)}), bf16[32,72,739]{2,1,0:T(8,128)(2,1)}, u32[]{:S(2)}, u32[]{:S(2)}) async-start(bf16[32,72,739]{2,1,0:T(8,128)(2,1)} %scatter_fusion), calls=%async_computation | async-start | bytes 7077888 | tf_op jit(solution)/shard_map/all_to_all | solution.py:49
  121.6 35.3 %all-gather.2.cloned.1.call-start = ((), (), s32[]{:S(2)}) async-start(), calls=%async_computation.2 | async-start | bytes 1638400 | tf_op jit(solution)/shard_map/all_gather | solution.py:60
  122.7 183.0 %reduce-scatter.2.cloned.1.call-start = ((), (), s32[]{:S(2)}) async-start(), calls=%async_computation.3 | async-start | bytes 3276800 | tf_op jit(solution)/shard_map/reduce_scatter | solution.py:87
  156.9 9.2 %copy-start.1 = (bf16[1280,512]{1,0:T(8,128)(2,1)S(1)}, bf16[1280,512]{1,0:T(8,128)(2,1)}, u32[]{:S(2)}) copy-start(bf16[1280,512]{1,0:T(8,128)(2,1)} %all-gather.2.cloned.1.call-done) | copy-start | bytes 3932164
  173.6 28.0 %copy-start.14 = (bf16[512,227]{0,1:T(8,128)(2,1)S(1)}, bf16[512,227]{0,1:T(8,128)(2,1)}, u32[]{:S(2)}) copy-start(bf16[512,227]{0,1:T(8,128)(2,1)} %param.17) | copy-start | bytes 697348
  181.1 22.6 %copy-start.16 = (bf16[512,512]{1,0:T(8,128)(2,1)S(1)}, bf16[512,512]{1,0:T(8,128)(2,1)}, u32[]{:S(2)}) copy-start(bf16[512,512]{1,0:T(8,128)(2,1)} %param.15) | copy-start | bytes 1572868
  203.7 4.0 copy-start.5
  203.7 4.0 copy-start.6
  203.7 4.0 copy-start.7
  203.7 4.6 copy-start.8
  269.4 1.5 copy-start.2
  270.9 182.4 %all-reduce.3.cloned.1.call-start = ((), (), s32[]{:S(2)}) async-start(), calls=%async_computation.4 | async-start | bytes 7241728 | tf_op jit(solution)/shard_map/psum | solution.py:94
  275.9 5.0 %copy-start.4 = (bf16[2304,512]{1,0:T(8,128)(2,1)S(1)}, bf16[2304,512]{1,0:T(8,128)(2,1)}, u32[]{:S(2)}) copy-start(bf16[2304,512]{1,0:T(8,128)(2,1)} %get-tuple-element.30) | copy-start | bytes 7077892
  286.5 21.9 %copy-start.10 = (bf16[512,512]{1,0:T(8,128)(2,1)S(1)}, bf16[512,512]{1,0:T(8,128)(2,1)}, u32[]{:S(2)}) copy-start(bf16[512,512]{1,0:T(8,128)(2,1)} %param.14) | copy-start | bytes 1572868
  305.8 2.6 copy-start.3
  453.3 2.7 copy-start.13
  456.0 3.5 copy-start.12
Sparse Core Ops, SparseCore 0:
  124.5 32.3 all-gather.1
  271.0 34.7 reduce-scatter.1
  312.4 140.8 all-reduce.2
where the time goes:
time: 472 us; the launch traced here: 467 us
  waiting for transfers between devices  218 us (46%)
  local copies, waits for them, and re-layouts  134 us (28%)
  other arithmetic  58.8 us (12%)
  matrix products  35.1 us (7%)
  between operations  14 us (3%)
  starting transfers between devices  7.79 us (2%)
    psum x1, waiting for transfers between devices, shards(): mesh_total = lax.psum(mesh_part, ('band', 'sub'))  144 us
    scatter x1, local copies, waits for them, and re-layouts, shards(): jnp.zeros((devices, capacity, row_width), jnp.bfloat16)  102 us
    scatter-add x3, other arithmetic, shards(): node_part.at[local_node[corner]].add(pre_grads[corner].astype(jnp.float32))  51.9 us
    all_gather x1, waiting for transfers between devices, shards(): patch_proj = lax.all_gather(mesh_proj, 'sub', axis=0, tiled=True)  33.9 us
    gather x3, local copies, waits for them, and re-layouts, shards(): patch_proj[local_node[corner]].astype(jnp.float32) + grid_float  24.2 us
    all_to_all x1, waiting for transfers between devices, shards(): lax.all_to_all(send_buffer, ('band', 'sub'), split_axis=0, concat_axis=0,...  20.5 us
    reduce_scatter x1, waiting for transfers between devices, shards(): lax.psum_scatter(node_part, 'sub', scatter_dimension=0, tiled=True)  19.3 us
    dot_general x4, matrix products, contract_rows(): lax.dot_general(left, right, (((0,), (0,)), ((), ())), preferred_element_...  17.9 us
  transfers between devices with their start and end apart: 4, of which 4 were waited for; matrix products, arithmetic and copies ran while one was open for 9% of the time, Pallas kernels for 0%

commit v1 on v0

--- a/solution.py
+++ b/solution.py
@@ -3,6 +3,7 @@
 import jax.numpy as jnp
 from jax import lax
 from jax.sharding import PartitionSpec as P
+from jax.lax import psum
 
 
 def latitude_weight(points, total):
@@ -91,7 +92,7 @@
     mesh_part = contract_rows(mesh_latent, mesh_proj_grad)
     grad_scale = 1.0 / math.sqrt(3.0 * total_points)
     grid_total = lax.psum(grid_part, ("band", "sub"))
-    mesh_total = lax.psum(mesh_part, ("band", "sub"))
+    mesh_total = psum(psum(mesh_part, "sub"), axis_name="band")
     return (
         mesh_grad,
         mesh_total * grad_scale,

time: 472 us -> 583 us (1.24)
  waiting for transfers between devices: 218 us -> 328 us
    psum x1 -> x3, waiting for transfers between devices: 144 us -> 245 us  [the longest x1 144 us: shards(): grid_total = lax.psum(grid_part, ('band', 'sub'))]
    reduce_scatter x1, waiting for transfers between devices: 19.3 us -> 28.6 us  [shards(): lax.psum_scatter(node_part, 'sub', scatter_dimension=0, tiled=True)]
  transfers between devices with their start and end apart: 4 -> 6, of which waited for: 4 -> 6; matrix products, arithmetic and copies ran while one was open for 9% -> 8% of each run, Pallas kernels for 0% -> 0%
where the time goes in v1:
time: 583 us; the launch traced here: 579 us
  waiting for transfers between devices  328 us (56%)
  local copies, waits for them, and re-layouts  134 us (23%)
  other arithmetic  60.1 us (10%)
  matrix products  34.8 us (6%)
  between operations  14 us (2%)
  starting transfers between devices  7.7 us (1%)
    psum x1, waiting for transfers between devices, shards(): grid_total = lax.psum(grid_part, ('band', 'sub'))  144 us
    scatter x1, local copies, waits for them, and re-layouts, shards(): jnp.zeros((devices, capacity, row_width), jnp.bfloat16)  101 us
    psum x2, waiting for transfers between devices, shards(): mesh_total = psum(psum(mesh_part, 'sub'), axis_name='band')  101 us
    scatter-add x3, other arithmetic, shards(): node_part.at[local_node[corner]].add(pre_grads[corner].astype(jnp.float32))  51.9 us
    all_gather x1, waiting for transfers between devices, shards(): patch_proj = lax.all_gather(mesh_proj, 'sub', axis=0, tiled=True)  33.9 us
    reduce_scatter x1, waiting for transfers between devices, shards(): lax.psum_scatter(node_part, 'sub', scatter_dimension=0, tiled=True)  28.6 us
    gather x3, local copies, waits for them, and re-layouts, shards(): patch_proj[local_node[corner]].astype(jnp.float32) + grid_float  24.2 us
    all_to_all x1, waiting for transfers between devices, shards(): lax.all_to_all(send_buffer, ('band', 'sub'), split_axis=0, concat_axis=0,...  20.5 us
  transfers between devices with their start and end apart: 6, of which 6 were waited for; matrix products, arithmetic and copies ran while one was open for 8% of the time, Pallas kernels for 0%

profile of v1, /device:TPU:0, one launch (start us, length us, event | category | flops | bytes accessed | tf_op | source)
XLA Modules:
  0.0 579.0 jit_solution(12901763216712008063)
XLA Ops:
  9.2 1.2 pad_maximum_fusion
  10.5 2.0 broadcast_in_dim.9
  12.5 101.4 %scatter_fusion = bf16[32,72,739]{2,1,0:T(8,128)(2,1)} fusion(bf16[32,72,739]{2,1,0:T(8,128)(2,1)} %broadcast_in_dim.9, s32[768]{0:T(1024)S(1)} %fusion.23, bf16[768,739]{1,0:T(8,128)(2,1)S(1)} %pad_maximum_fusion), kind=kCustom, calls=%fused_computation.3 | custom fusion | bytes 3411456 | tf_op jit(solution)/shard_map/scatter | solution.py:48
  114.0 7.5 %all-to-all-start = ((bf16[32,72,739]{2,1,0:T(8,128)(2,1)}), bf16[32,72,739]{2,1,0:T(8,128)(2,1)}, u32[]{:S(2)}, u32[]{:S(2)}) async-start(bf16[32,72,739]{2,1,0:T(8,128)(2,1)} %scatter_fusion), calls=%async_computation | async-start | bytes 7077888 | tf_op jit(solution)/shard_map/all_to_all | solution.py:50
  121.5 1.1 convolution_convert_fusion.4
  122.8 33.9 %all-gather.2.cloned.1.call-done = bf16[1280,512]{1,0:T(8,128)(2,1)} async-done(((bf16[320,512]{1,0:T(8,128)(2,1)}), bf16[1280,512]{1,0:T(8,128)(2,1)}) %all-gather.2.cloned.1.call-update) | async-done | bytes 1310736 | tf_op jit(solution)/shard_map/all_gather | solution.py:61
  156.8 9.2 %gather_fusion.2 = bf16[2304,512]{1,0:T(8,128)(2,1)} fusion(bf16[1280,512]{1,0:T(8,128)(2,1)} %all-gather.2.cloned.1.call-done, s32[3072]{0:T(1024)S(1)} %get-tuple-element.32), kind=kCustom, calls=%fused_computation.2 | custom fusion | bytes 4727808 | tf_op jit(solution)/shard_map/gather | solution.py:67
  166.0 7.5 %gather_fusion.1 = bf16[2304,512]{1,0:T(8,128)(2,1)} fusion(bf16[1280,512]{1,0:T(8,128)(2,1)S(1)} %copy-done.1, s32[3072]{0:T(1024)S(1)} %get-tuple-element.33), kind=kCustom, calls=%fused_computation.1 | custom fusion | bytes 4727808 | tf_op jit(solution)/shard_map/gather | solution.py:67
  173.5 7.5 %gather_fusion = bf16[2304,512]{1,0:T(8,128)(2,1)} fusion(bf16[1280,512]{1,0:T(8,128)(2,1)S(1)} %copy-done.1, s32[3072]{0:T(1024)S(1)} %pad_clamp_fusion.2), kind=kCustom, calls=%fused_computation | custom fusion | bytes 4727808 | tf_op jit(solution)/shard_map/gather | solution.py:67
  181.0 20.5 %all-to-all-done = bf16[32,72,739]{2,1,0:T(8,128)(2,1)} async-done(((bf16[32,72,739]{2,1,0:T(8,128)(2,1)}), bf16[32,72,739]{2,1,0:T(8,128)(2,1)}, u32[]{:S(2)}, u32[]{:S(2)}) %all-to-all-start) | async-done | bytes 3405344 | tf_op jit(solution)/shard_map/all_to_all | solution.py:50
  201.5 2.0 convolution_convert_fusion.2
  203.6 3.9 convolution_convert_fusion.1
  208.2 9.1 %multiply_convert_fusion = (bf16[2304,512]{1,0:T(8,128)(2,1)}, bf16[2304,512]{1,0:T(8,128)(2,1)}, bf16[2304,512]{1,0:T(8,128)(2,1)}, bf16[2304,512]{1,0:T(8,128)(2,1)}) fusion(bf16[2304,512]{1,0:T(8,128)(2,1)S(1)} %convolution_convert_fusion.1, bf16[2304,512]{1,0:T(8,128)(2,1)S(1)} %copy-done.6, bf16[2304,512]{1,0:T(8,128)(2,1)S(1)} %copy-done.7, ...), kind=kOutput, calls=%fused_computation.20 | convolution fusion | flops 1255145472 | bytes 21757952 | tf_op jit(solution)/shard_map/dot_general | solution.py:26
  217.3 17.0 %scatter_custom_fusion.1 = f32[1280,512]{1,0:T(8,128)S(1)} fusion(s32[2304]{0:T(1024)S(1)} %get-tuple-element.22, bf16[2304,512]{1,0:T(8,128)(2,1)} %get-tuple-element.29, f32[]{:T(128)} %constant.20.clone.1), kind=kCustom, calls=%fused_computation.16 | custom fusion | flops 2359296 | bytes 4980740 | tf_op jit(solution)/shard_map/scatter-add | solution.py:87
  234.3 17.5 %scatter_custom_fusion.2 = f32[1280,512]{1,0:T(8,128)S(1)} fusion(f32[1280,512]{1,0:T(8,128)S(1)} %scatter_custom_fusion.1, s32[2304]{0:T(1024)S(1)} %get-tuple-element.21, bf16[2304,512]{1,0:T(8,128)(2,1)} %get-tuple-element.27), kind=kCustom, calls=%fused_computation.14 | custom fusion | flops 2359296 | bytes 4980736 | tf_op jit(solution)/shard_map/scatter-add | solution.py:87
  251.9 17.4 %scatter_custom_fusion.3 = f32[1280,512]{1,0:T(8,128)S(1)} fusion(f32[1280,512]{1,0:T(8,128)S(1)} %scatter_custom_fusion.2, s32[2304]{0:T(1024)S(1)} %get-tuple-element.20, bf16[2304,512]{1,0:T(8,128)(2,1)} %get-tuple-element.26), kind=kCustom, calls=%fused_computation.11 | custom fusion | flops 2359296 | bytes 4980736 | tf_op jit(solution)/shard_map/scatter-add | solution.py:87
  269.2 1.5 copy-done.2
  270.8 6.2 %fusion.7 = f32[512,512]{0,1:T(8,128)} fusion(bf16[2304,512]{1,0:T(8,128)(2,1)} %get-tuple-element.26, bf16[2304,512]{1,0:T(8,128)(2,1)} %get-tuple-element.27, bf16[2304,512]{1,0:T(8,128)(2,1)} %get-tuple-element.29, bf16[2304,739]{1,0:T(8,128)(2,1)} %bitcast.2), kind=kOutput, calls=%fused_computation.29 | convolution fusion | flops 1215037440 | bytes 10485760 | tf_op jit(solution)/shard_map/dot_general | solution.py:20
  277.0 28.6 %reduce-scatter.2.cloned.1.call-done = f32[320,512]{1,0:T(8,128)} async-done(((f32[1280,512]{1,0:T(8,128)}), f32[320,512]{1,0:T(8,128)}) %reduce-scatter.2.cloned.1.call-update) | async-done | bytes 655376 | tf_op jit(solution)/shard_map/reduce_scatter | solution.py:88
  305.7 2.5 convolution_bitcast_fusion
  308.3 4.1 fusion.24
  312.3 4.9 fusion.12
  317.3 27.7 %all-reduce.5.cloned.1.call-done = f32[512,512]{0,1:T(8,128)} async-done(((f32[512,512]{0,1:T(8,128)}), f32[512,512]{0,1:T(8,128)}) %all-reduce.5.cloned.1.call-update) | async-done | bytes 1048592 | tf_op jit(solution)/shard_map/psum | solution.py:95
  345.0 143.9 %all-reduce.9.cloned.1.call-done = (f32[512,512]{0,1:T(8,128)}, f32[512,512]{0,1:T(8,128)}, f32[512,227]{0,1:T(8,128)}) async-done(((f32[512,512]{0,1:T(8,128)}, f32[512,512]{0,1:T(8,128)}, f32[512,227]{0,1:T(8,128)}), (f32[512,512]{0,1:T(8,128)}, f32[512,512]{0,1:T(8,128)}, f32[512,227]{0,1:T(8,128)})) %all-reduce.9.cloned.1.call-update) | async-done | bytes 2562064 | tf_op jit(solution)/shard_map/psum | solution.py:94
  488.9 1.3 broadcast_multiply_fusion.1
  490.2 1.3 copy.30
  491.5 1.5 broadcast_multiply_fusion
  493.0 1.3 copy.31
  495.1 1.1 convolution_convert_fusion.3
  496.2 73.6 %all-reduce.7.cloned.1.call-done = f32[512,512]{0,1:T(8,128)} async-done(((f32[512,512]{0,1:T(8,128)}), f32[512,512]{0,1:T(8,128)}) %all-reduce.7.cloned.1.call-update) | async-done | bytes 1048592 | tf_op jit(solution)/shard_map/psum | solution.py:95
  569.8 1.3 broadcast_multiply_fusion.2
  571.1 1.3 copy.29
  (51 shorter events, 4.0 us)
Async XLA Ops:
  7.2 200.4 %copy-start = (bf16[512,512]{1,0:T(8,128)(2,1)S(1)}, bf16[512,512]{1,0:T(8,128)(2,1)}, u32[]{:S(2)}) copy-start(bf16[512,512]{1,0:T(8,128)(2,1)} %param.16) | copy-start | bytes 1572868
  113.9 7.6 %copy-start.9 = (bf16[512,512]{1,0:T(8,128)(2,1)S(1)}, bf16[512,512]{1,0:T(8,128)(2,1)}, u32[]{:S(2)}) copy-start(bf16[512,512]{1,0:T(8,128)(2,1)} %param.14) | copy-start | bytes 1572868
  113.9 7.6 %copy-start.11 = (bf16[320,512]{1,0:T(8,128)(2,1)S(1)}, bf16[320,512]{1,0:T(8,128)(2,1)}, u32[]{:S(2)}) copy-start(bf16[320,512]{1,0:T(8,128)(2,1)} %param.11) | copy-start | bytes 983044
  113.9 8.7 %copy-start.14 = (s32[3,2304]{1,0:T(4,128)S(1)}, s32[3,2304]{1,0:T(4,128)}, u32[]{:S(2)}) copy-start(s32[3,2304]{1,0:T(4,128)} %param.13) | copy-start | bytes 82948
  114.0 87.6 %all-to-all-start = ((bf16[32,72,739]{2,1,0:T(8,128)(2,1)}), bf16[32,72,739]{2,1,0:T(8,128)(2,1)}, u32[]{:S(2)}, u32[]{:S(2)}) async-start(bf16[32,72,739]{2,1,0:T(8,128)(2,1)} %scatter_fusion), calls=%async_computation | async-start | bytes 7077888 | tf_op jit(solution)/shard_map/all_to_all | solution.py:50
  121.5 35.3 %all-gather.2.cloned.1.call-start = ((), (), s32[]{:S(2)}) async-start(), calls=%async_computation.2 | async-start | bytes 1638400 | tf_op jit(solution)/shard_map/all_gather | solution.py:61
  122.6 183.1 %reduce-scatter.2.cloned.1.call-start = ((), (), s32[]{:S(2)}) async-start(), calls=%async_computation.3 | async-start | bytes 3276800 | tf_op jit(solution)/shard_map/reduce_scatter | solution.py:88
  156.8 9.2 %copy-start.1 = (bf16[1280,512]{1,0:T(8,128)(2,1)S(1)}, bf16[1280,512]{1,0:T(8,128)(2,1)}, u32[]{:S(2)}) copy-start(bf16[1280,512]{1,0:T(8,128)(2,1)} %all-gather.2.cloned.1.call-done) | copy-start | bytes 3932164
  173.5 28.0 %copy-start.13 = (bf16[512,227]{0,1:T(8,128)(2,1)S(1)}, bf16[512,227]{0,1:T(8,128)(2,1)}, u32[]{:S(2)}) copy-start(bf16[512,227]{0,1:T(8,128)(2,1)} %param.17) | copy-start | bytes 697348
  181.0 22.6 %copy-start.15 = (bf16[512,512]{1,0:T(8,128)(2,1)S(1)}, bf16[512,512]{1,0:T(8,128)(2,1)}, u32[]{:S(2)}) copy-start(bf16[512,512]{1,0:T(8,128)(2,1)} %param.15) | copy-start | bytes 1572868
  203.6 4.0 copy-start.4
  203.6 4.0 copy-start.6
  203.6 4.0 copy-start.7
  203.6 4.6 copy-start.8
  269.2 1.5 copy-start.2
  270.8 74.2 %all-reduce.5.cloned.1.call-start = ((), (), s32[]{:S(2)}) async-start(), calls=%async_computation.4 | async-start | bytes 2097152 | tf_op jit(solution)/shard_map/psum | solution.py:95
  277.0 31.2 %copy-start.5 = (bf16[2304,512]{1,0:T(8,128)(2,1)S(1)}, bf16[2304,512]{1,0:T(8,128)(2,1)}, u32[]{:S(2)}) copy-start(bf16[2304,512]{1,0:T(8,128)(2,1)} %copy-done.4) | copy-start | bytes 7077892
  308.2 180.7 %all-reduce.9.cloned.1.call-start = ((), (), s32[]{:S(2)}) async-start(), calls=%async_computation.6 | async-start | bytes 5144576 | tf_op jit(solution)/shard_map/psum | solution.py:94
  317.2 252.6 %all-reduce.7.cloned.1.call-start = ((), (), s32[]{:S(2)}) async-start(), calls=%async_computation.5 | async-start | bytes 2097152 | tf_op jit(solution)/shard_map/psum | solution.py:95
  491.5 2.8 copy-start.12
  491.5 3.6 copy-start.3
  491.5 3.6 copy-start.10
Sparse Core Ops, SparseCore 0:
  124.4 32.3 all-gather.1
  270.9 34.7 reduce-scatter.1
  308.6 36.2 all-reduce.4
  351.3 137.5 all-reduce.8
  492.2 77.5 all-reduce.6
